TPU v7x, 8 devices: a whole 2x2x1 slice. The times are simulated.
8 devices in a mesh: data: 1 (over z), tp: 2 (over y), cp: 4 (over x, core).
Axes of the slice: x: 2, y: 2, z: 1, core: 2. Of those that a mesh axis runs over, the one named last changes fastest.
Arguments:
- x: bfloat16 [16, 1024, 5120], P('data', ('cp', 'tp'))
- positions: int32 [16, 1024], P('data', ('cp', 'tp'))
- w_query: bfloat16 [5120, 5120], P(None, 'tp')
- w_key: bfloat16 [5120, 1024], P(None, 'tp')
- w_value: bfloat16 [5120, 1024], P(None, 'tp')
- w_out: bfloat16 [5120, 5120], P('tp')
Outputs:
- output: bfloat16 [16, 1024, 5120], P('data', ('cp', 'tp'))
All inputs are finite; a program needn't handle non-finite values.
Results may differ from a plain program's by a relative error of at most 0.00658.
Values are sent between devices in bfloat16 or wider.
A program may use at most 1 GiB of HBM per device.

v0:
```python
import math
import jax
import jax.numpy as jnp
from jax import lax
from jax.sharding import PartitionSpec as P

HEAD_DIM = 128
ROPE_BASE = 500000


def rope_tables(pos_vals):
    inv_freq = jnp.asarray([ROPE_BASE ** (-2.0 * freq_idx / HEAD_DIM) for freq_idx in range(HEAD_DIM // 2)], dtype=jnp.float32)
    angles = pos_vals.astype(jnp.float32)[..., None] * inv_freq
    return jnp.cos(angles), jnp.sin(angles)


def apply_rope(head_vals, cos_t, sin_t):
    half_dim = head_vals.shape[-1] // 2
    lower_half = head_vals[..., :half_dim]
    upper_half = head_vals[..., half_dim:]
    return jnp.concatenate([lower_half * cos_t - upper_half * sin_t, upper_half * cos_t + lower_half * sin_t], axis=-1)


def project_heads(x_rows, pos_rows, w_query, w_key, w_value):
    batch_rows, n_rows = pos_rows.shape
    kv_local = w_key.shape[1] // HEAD_DIM
    q_per_kv = w_query.shape[1] // w_key.shape[1]
    cos_t, sin_t = rope_tables(pos_rows)
    q_proj = jnp.dot(x_rows, w_query, preferred_element_type=jnp.float32).astype(jnp.bfloat16)
    k_proj = jnp.dot(x_rows, w_key, preferred_element_type=jnp.float32).astype(jnp.bfloat16)
    v_proj = jnp.dot(x_rows, w_value, preferred_element_type=jnp.float32).astype(jnp.bfloat16)
    q_heads = q_proj.reshape(batch_rows, n_rows, kv_local, q_per_kv, HEAD_DIM).astype(jnp.float32)
    q_rot = apply_rope(q_heads, cos_t[:, :, None, None, :], sin_t[:, :, None, None, :]).astype(jnp.bfloat16)
    k_heads = k_proj.reshape(batch_rows, n_rows, kv_local, HEAD_DIM).astype(jnp.float32)
    k_rot = apply_rope(k_heads, cos_t[:, :, None, :], sin_t[:, :, None, :]).astype(jnp.bfloat16)
    return q_rot, k_rot, v_proj.reshape(batch_rows, n_rows, kv_local, HEAD_DIM)


def block_scores(q_blk, k_blk):
    return jnp.einsum('bqhgd,bkhd->bhgqk', q_blk, k_blk, preferred_element_type=jnp.float32) * (1.0 / math.sqrt(HEAD_DIM))


def masked_scores(q_blk, k_blk, qpos_blk, kpos_blk):
    visible = kpos_blk[:, None, None, None, :] <= qpos_blk[:, None, None, :, None]
    return jnp.where(visible, block_scores(q_blk, k_blk), -jnp.inf)


def start_state(scores, v_blk):
    row_max = scores.max(axis=-1)
    exp_scores = jnp.exp(scores - row_max[..., None])
    out_accum = jnp.einsum('bhgqk,bkhd->bhgqd', exp_scores.astype(jnp.bfloat16), v_blk, preferred_element_type=jnp.float32)
    return row_max, exp_scores.sum(axis=-1), out_accum


def absorb(soft_state, scores, v_blk):
    run_max, run_sum, out_accum = soft_state
    new_max = jnp.maximum(run_max, scores.max(axis=-1))
    rescale = jnp.exp(run_max - new_max)
    exp_scores = jnp.exp(scores - new_max[..., None])
    new_sum = run_sum * rescale + exp_scores.sum(axis=-1)
    new_accum = out_accum * rescale[..., None] + jnp.einsum('bhgqk,bkhd->bhgqd', exp_scores.astype(jnp.bfloat16), v_blk, preferred_element_type=jnp.float32)
    return new_max, new_sum, new_accum


def finish(soft_state):
    run_sum = soft_state[1]
    return (soft_state[2] / run_sum[..., None]).astype(jnp.bfloat16)


def project_out(attn_out, w_out):
    w_out_heads = w_out.reshape(attn_out.shape[1], attn_out.shape[2], HEAD_DIM, w_out.shape[1])
    return jnp.einsum('bhgqd,hgde->bqe', attn_out, w_out_heads, preferred_element_type=jnp.float32)


def solution(mesh):
    cp_size = mesh.shape['cp']
    send_pairs = [(src_dev, (src_dev + 1) % cp_size) for src_dev in range(cp_size)]
    row_spec = P('data', ('cp', 'tp'))

    def local_fn(x_rows, pos_rows, w_query, w_key, w_value, w_out):
        x_pair = lax.all_gather(x_rows, 'tp', axis=1, tiled=True)
        pos_pair = lax.all_gather(pos_rows, 'tp', axis=1, tiled=True)
        half_len = x_pair.shape[1] // 2
        q_rot, k_rot, v_heads = project_heads(x_pair, pos_pair, w_query, w_key, w_value)
        q_low = q_rot[:, :half_len]
        q_high = q_rot[:, half_len:]
        pos_low = pos_pair[:, :half_len]
        pos_high = pos_pair[:, half_len:]
        low_state = start_state(masked_scores(q_low, k_rot[:, :half_len], pos_low, pos_low), v_heads[:, :half_len])
        high_state = start_state(masked_scores(q_high, k_rot, pos_high, pos_pair), v_heads)
        my_index = lax.axis_index('cp')

        def source_below(low_state, high_state, kv_blk):
            k_first = kv_blk[0][:, :half_len]
            v_first = kv_blk[1][:, :half_len]
            return (absorb(low_state, block_scores(q_low, k_first), v_first),
                    absorb(high_state, block_scores(q_high, k_first), v_first))

        def source_above(low_state, high_state, kv_blk):
            return low_state, absorb(high_state, block_scores(q_high, kv_blk[0]), kv_blk[1])

        def kv_step(step_idx, loop_carry):
            kv_blk, low_state, high_state = loop_carry
            kv_blk = lax.ppermute(kv_blk, 'cp', send_pairs)
            source = (my_index - step_idx) % cp_size
            low_state, high_state = lax.cond(source < my_index, source_below, source_above, low_state, high_state, kv_blk)
            return kv_blk, low_state, high_state

        kv_own = jnp.stack([k_rot, v_heads])
        _, low_state, high_state = lax.fori_loop(1, cp_size, kv_step, (kv_own, low_state, high_state))
        attn_out = jnp.concatenate([finish(low_state), finish(high_state)], axis=3)
        partial_y = project_out(attn_out, w_out)
        y_rows = lax.psum_scatter(partial_y, 'tp', scatter_dimension=1, tiled=True)
        return (x_rows.astype(jnp.float32) + y_rows).astype(jnp.bfloat16)

    return jax.shard_map(local_fn, mesh=mesh,
                         in_specs=(row_spec, row_spec, P(None, 'tp'), P(None, 'tp'), P(None, 'tp'), P('tp', None)),
                         out_specs=row_spec, check_vma=False)
```

profile of v0, /device:TPU:0, one launch (start us, length us, event | category | flops | bytes accessed | tf_op | source)
XLA Modules:
  0.0 2714.6 jit_solution(13705466746547869292)
XLA Ops:
  24.2 468.8 %all-gather.2.cloned.1.call-done = bf16[16,256,5120]{2,1,0:T(8,128)(2,1)} async-done(((bf16[16,128,5120]{2,1,0:T(8,128)(2,1)}), bf16[16,256,5120]{2,1,0:T(8,128)(2,1)}) %all-gather.2.cloned.1.call-update) | async-done | bytes 41943056 | tf_op jit(solution)/shard_map/all_gather | solution.py:81
  493.0 28.8 %fusion.77 = bf16[16,256,512]{2,1,0:T(8,128)(2,1)} fusion(bf16[16,256,5120]{2,1,0:T(8,128)(2,1)} %all-gather.2.cloned.1.call-done, bf16[5120,512]{1,0:T(8,128)(2,1)} %param.15), kind=kOutput, calls=%fused_computation.104 | convolution fusion | flops 21476933632 | bytes 51380224 | tf_op jit(solution)/shard_map/dot_general | solution.py:31
  541.0 29.2 %convert_convert_fusion.1 = f32[16,256,512]{2,1,0:T(8,128)} fusion(bf16[16,256,5120]{2,1,0:T(8,128)(2,1)} %all-gather.2.cloned.1.call-done, bf16[5120,512]{1,0:T(8,128)(2,1)} %param.14), kind=kOutput, calls=%fused_computation.97 | convolution fusion | flops 21479030784 | bytes 55574528 | tf_op jit(solution)/shard_map/dot_general | solution.py:30
  594.3 122.3 %convert_convert_fusion = f32[16,256,2560]{2,1,0:T(8,128)} fusion(bf16[16,256,5120]{2,1,0:T(8,128)(2,1)} %all-gather.2.cloned.1.call-done, bf16[5120,2560]{1,0:T(8,128)(2,1)} %param.13), kind=kOutput, calls=%fused_computation.75 | convolution fusion | flops 107395153920 | bytes 110100480 | tf_op jit(solution)/shard_map/dot_general | solution.py:29
  716.5 38.8 %copy.31 = f32[16,256,2560]{1,2,0:T(8,128)} copy(f32[16,256,2560]{2,1,0:T(8,128)} %convert_convert_fusion) | data formatting | bytes 83886080 | tf_op jit(solution)/shard_map/convert_element_type | solution.py:32
  755.4 29.0 %fusion.91 = (f32[16,256,4,5,64]{1,4,3,2,0:T(8,128)}, f32[16,256,4,5,64]{1,4,3,2,0:T(8,128)}) fusion(f32[16,256,4,5,128]{1,4,3,2,0:T(8,128)} %bitcast.148), kind=kLoop, calls=%fused_computation.118 | loop fusion | bytes 83886080 | tf_op jit(solution)/shard_map/slice | solution.py:19
  784.4 28.3 %copy.65 = f32[16,256,4,5,64]{4,1,3,2,0:T(8,128)} copy(f32[16,256,4,5,64]{1,4,3,2,0:T(8,128)} %get-tuple-element.406) | data formatting | bytes 41943040
  812.7 28.5 %copy.66 = f32[16,256,4,5,64]{4,1,3,2,0:T(8,128)} copy(f32[16,256,4,5,64]{1,4,3,2,0:T(8,128)} %get-tuple-element.407) | data formatting | bytes 41943040
  851.9 36.1 %add_convert_fusion.1 = (bf16[16,256,4,5,64]{4,1,3,2,0:T(8,128)(2,1)S(1)}, bf16[16,256,4,5,64]{4,1,3,2,0:T(8,128)(2,1)}) fusion(f32[16,256,4,5,64]{4,1,3,2,0:T(8,128)} %copy.65, f32[16,256,4,5,64]{4,1,3,2,0:T(8,128)} %copy.66, f32[16,256,64]{2,1,0:T(8,128)} %get-tuple-element.413, f32[16,256,64]{2,1,0:T(8,128)} %get-tuple-element.412), kind=kLoop, calls=%fused_computation.51 | loop fusion | flops 41943040 | bytes 65011712 | tf_op jit(solution)/shard_map/convert.3
  888.0 20.8 pad_maximum_fusion
  908.8 17.3 fusion.59
  950.3 25.6 fusion.39
  975.9 17.9 fusion.38
  993.8 27.7 %fusion.44 = f32[16,4,5,128,128]{4,3,2,1,0:T(8,128)} fusion(f32[16,4,256,128,5]{3,2,4,1,0:T(8,128)} %get-tuple-element.419, f32[16,4,5,128]{3,2,1,0:T(8,128)S(1)} %get-tuple-element.518, pred[16,128,256]{1,2,0:T(8,128)(4,1)S(1)} %copy-done.6, bf16[16,256,4,128,1]{3,2,1,0,4:T(4,128)(2,1)} %bitcast.151), kind=kOutput, calls=%fused_computation.60 | convolution fusion | flops 2726297600 | bytes 67796992 | tf_op jit(solution)/shard_map/bhgqk,bkhd->bhgqd/dot_general | solution.py:51
  1029.9 575.6 %while.27 = (s32[]{:T(128)}, bf16[2,16,256,4,128]{4,2,3,1,0:T(8,128)(2,1)}, f32[16,4,5,128]{3,2,1,0:T(8,128)S(1)}, f32[16,4,5,128]{3,2,1,0:T(8,128)S(1)}, f32[16...) while((s32[]{:T(128)}, ...), condition=%wide.region_13.14_spmd, body=%wide.region_4.13_spmd.sunk | while | flops 5473730560 | bytes 328499712 | solution.py:110
  1030.1 92.8 %collective-permute-done = bf16[2,16,256,4,128]{4,2,3,1,0:T(8,128)(2,1)} collective-permute-done((bf16[2,16,256,4,128]{4,2,3,1,0:T(8,128)(2,1)}, bf16[2,16,256,4,128]{4,2,3,1,0:T(8,128)(2,1)}, u32[]{:S(2)}, u32[]{:S(2)}) %collective-permute-start) | collective-permute-done | bytes 8388640 | tf_op jit(solution)/shard_map/while/body/eval_jaxpr/ppermute | solution.py:104
  1122.9 70.8 %conditional.2 = (f32[16,4,5,128]{3,2,1,0:T(8,128)S(1)}, f32[16,4,5,128]{3,2,1,0:T(8,128)S(1)}, f32[16,4,5,128,128]{4,3,2,1,0:T(8,128)}, f32[16,4,5,128]{3,2,1,0...) conditional(s32[]{:T(128)} %convert_element_type.112, ...), branch_computations={%region_5.7_spmd, %region_8.12_spmd} | conditional | flops 5473730560 | bytes 277839936 | solution.py:106
  1122.9 21.1 bitcast_reduce_fusion
  1162.9 30.8 %multiply_add_fusion = f32[16,4,5,128,128]{4,3,2,1,0:T(8,128)} fusion(f32[16,4,5,128,128]{4,3,2,1,0:T(8,128)} %get-tuple-element.328, f32[16,4,5,128]{3,2,1,0:T(8,128)S(1)} %get-tuple-element.387, f32[16,4,256,128,5]{3,2,4,1,0:T(8,128)} %get-tuple-element.393, f32[16,4,5,128]{3,2,1,0:T(8,128)} %max.6, bf16[2,16,256,4,128]{4,2,3,1,0:T(8,128)(2,1)} %get-tuple-element.325), kind=kOutput, calls=%fused_computation.6 | convolution fusion | flops 2726297600 | bytes 88506368 | tf_op jit(solution)/shard_map/while/body/eval_jaxpr/cond/branch_0_fun/bhgqk,bkhd->bhgqd/dot_general | solution.py:61
  1202.4 30.7 %collective-permute-start = (bf16[2,16,256,4,128]{4,2,3,1,0:T(8,128)(2,1)}, bf16[2,16,256,4,128]{4,2,3,1,0:T(8,128)(2,1)}, u32[]{:S(2)}, u32[]{:S(2)}) collective-permute-start(bf16[2,16,256,4,128]{4,2,3,1,0:T(8,128)(2,1)} %get-tuple-element.529), channel_id=1, source_target_pairs={{0,1},{1,2},{2,3},{3,0},{4,5},{5,6},{6,7},{7,4}} | collective-permute-start | bytes 25165832 | tf_op jit(solution)/shard_map/while/body/eval_jaxpr/ppermute | solution.py:104
  1233.0 91.3 %collective-permute-done = bf16[2,16,256,4,128]{4,2,3,1,0:T(8,128)(2,1)} collective-permute-done((bf16[2,16,256,4,128]{4,2,3,1,0:T(8,128)(2,1)}, bf16[2,16,256,4,128]{4,2,3,1,0:T(8,128)(2,1)}, u32[]{:S(2)}, u32[]{:S(2)}) %collective-permute-start) | collective-permute-done | bytes 8388640 | tf_op jit(solution)/shard_map/while/body/eval_jaxpr/ppermute | solution.py:104
  1324.3 70.8 %conditional.2 = (f32[16,4,5,128]{3,2,1,0:T(8,128)S(1)}, f32[16,4,5,128]{3,2,1,0:T(8,128)S(1)}, f32[16,4,5,128,128]{4,3,2,1,0:T(8,128)}, f32[16,4,5,128]{3,2,1,0...) conditional(s32[]{:T(128)} %convert_element_type.112, ...), branch_computations={%region_5.7_spmd, %region_8.12_spmd} | conditional | flops 5473730560 | bytes 277839936 | solution.py:106
  1324.3 21.1 bitcast_reduce_fusion
  1364.3 30.8 %multiply_add_fusion = f32[16,4,5,128,128]{4,3,2,1,0:T(8,128)} fusion(f32[16,4,5,128,128]{4,3,2,1,0:T(8,128)} %get-tuple-element.328, f32[16,4,5,128]{3,2,1,0:T(8,128)S(1)} %get-tuple-element.387, f32[16,4,256,128,5]{3,2,4,1,0:T(8,128)} %get-tuple-element.393, f32[16,4,5,128]{3,2,1,0:T(8,128)} %max.6, bf16[2,16,256,4,128]{4,2,3,1,0:T(8,128)(2,1)} %get-tuple-element.325), kind=kOutput, calls=%fused_computation.6 | convolution fusion | flops 2726297600 | bytes 88506368 | tf_op jit(solution)/shard_map/while/body/eval_jaxpr/cond/branch_0_fun/bhgqk,bkhd->bhgqd/dot_general | solution.py:61
  1405.4 120.3 %collective-permute-done = bf16[2,16,256,4,128]{4,2,3,1,0:T(8,128)(2,1)} collective-permute-done((bf16[2,16,256,4,128]{4,2,3,1,0:T(8,128)(2,1)}, bf16[2,16,256,4,128]{4,2,3,1,0:T(8,128)(2,1)}, u32[]{:S(2)}, u32[]{:S(2)}) %collective-permute-start) | collective-permute-done | bytes 8388640 | tf_op jit(solution)/shard_map/while/body/eval_jaxpr/ppermute | solution.py:104
  1525.8 70.8 %conditional.2 = (f32[16,4,5,128]{3,2,1,0:T(8,128)S(1)}, f32[16,4,5,128]{3,2,1,0:T(8,128)S(1)}, f32[16,4,5,128,128]{4,3,2,1,0:T(8,128)}, f32[16,4,5,128]{3,2,1,0...) conditional(s32[]{:T(128)} %convert_element_type.112, ...), branch_computations={%region_5.7_spmd, %region_8.12_spmd} | conditional | flops 5473730560 | bytes 277839936 | solution.py:106
  1525.8 21.1 bitcast_reduce_fusion
  1565.8 30.8 %multiply_add_fusion = f32[16,4,5,128,128]{4,3,2,1,0:T(8,128)} fusion(f32[16,4,5,128,128]{4,3,2,1,0:T(8,128)} %get-tuple-element.328, f32[16,4,5,128]{3,2,1,0:T(8,128)S(1)} %get-tuple-element.387, f32[16,4,256,128,5]{3,2,4,1,0:T(8,128)} %get-tuple-element.393, f32[16,4,5,128]{3,2,1,0:T(8,128)} %max.6, bf16[2,16,256,4,128]{4,2,3,1,0:T(8,128)(2,1)} %get-tuple-element.325), kind=kOutput, calls=%fused_computation.6 | convolution fusion | flops 2726297600 | bytes 88506368 | tf_op jit(solution)/shard_map/while/body/eval_jaxpr/cond/branch_0_fun/bhgqk,bkhd->bhgqd/dot_general | solution.py:61
  1605.5 21.2 fusion.49
  1626.7 118.1 %convolution_bitcast_fusion = f32[16,256,5120]{2,1,0:T(8,128)} fusion(bf16[4,5,128,5120,1]{3,2,1,0,4:T(8,128)(2,1)} %bitcast.152, bf16[16,4,5,128,128]{4,3,1,2,0:T(8,128)(2,1)} %get-tuple-element.420, bf16[16,4,5,128,128]{4,3,1,2,0:T(8,128)(2,1)} %get-tuple-element.421), kind=kOutput, calls=%fused_computation.47 | convolution fusion | flops 107416125440 | bytes 131072000 | tf_op jit(solution)/shard_map/bhgqd,hgde->bqe/dot_general | solution.py:72
  1744.8 935.1 %reduce-scatter.2.cloned.1.call-done = f32[16,128,5120]{2,1,0:T(8,128)} async-done(((f32[16,256,5120]{2,1,0:T(8,128)}), f32[16,128,5120]{2,1,0:T(8,128)}) %reduce-scatter.2.cloned.1.call-update) | async-done | bytes 41943056 | tf_op jit(solution)/shard_map/reduce_scatter | solution.py:113
  2679.9 27.5 %add_convert_fusion = bf16[16,128,5120]{2,1,0:T(8,128)(2,1)} fusion(f32[16,128,5120]{2,1,0:T(8,128)} %reduce-scatter.2.cloned.1.call-done, bf16[16,128,5120]{2,1,0:T(8,128)(2,1)} %param.11), kind=kLoop, calls=%fused_computation.49 | loop fusion | flops 31457280 | bytes 83886080 | tf_op jit(solution)/shard_map/convert_element_type | solution.py:114
  (56 shorter events, 188.5 us)
Async XLA Ops:
  6.5 8.9 copy-start.8
  6.5 0.8 copy-start.7
  6.5 486.5 %all-gather.2.cloned.1.call-start = ((), (), s32[]{:S(2)}) async-start(), calls=%async_computation.1 | async-start | bytes 62914560 | tf_op jit(solution)/shard_map/all_gather | solution.py:81
  7.3 2672.6 %reduce-scatter.2.cloned.1.call-start = ((), (), s32[]{:S(2)}) async-start(), calls=%async_computation.2 | async-start | bytes 125829120 | tf_op jit(solution)/shard_map/reduce_scatter | solution.py:113
  812.7 28.5 %copy-start.4 = (f32[16,256,64]{2,1,0:T(8,128)S(1)}, f32[16,256,64]{2,1,0:T(8,128)}, u32[]{:S(2)}) copy-start(f32[16,256,64]{2,1,0:T(8,128)} %get-tuple-element.412) | copy-start | bytes 3145732
  908.8 17.3 copy-start.5
  926.1 24.2 copy-start.2
  926.1 10.2 slice-start
  950.3 25.6 copy-start.6
  993.8 27.7 %copy-start.1 = (bf16[16,256,4,64]{3,1,2,0:T(8,128)(2,1)S(1)}, bf16[16,256,4,64]{3,1,2,0:T(8,128)(2,1)}, u32[]{:S(2)}) copy-start(bf16[16,256,4,64]{3,1,2,0:T(8,128)(2,1)} %get-tuple-element.408) | copy-start | bytes 6291460
  1021.4 8.4 copy-start.3
  1030.0 92.9 %collective-permute-start = (bf16[2,16,256,4,128]{4,2,3,1,0:T(8,128)(2,1)}, bf16[2,16,256,4,128]{4,2,3,1,0:T(8,128)(2,1)}, u32[]{:S(2)}, u32[]{:S(2)}) collective-permute-start(bf16[2,16,256,4,128]{4,2,3,1,0:T(8,128)(2,1)} %get-tuple-element.529), channel_id=1, source_target_pairs={{0,1},{1,2},{2,3},{3,0},{4,5},{5,6},{6,7},{7,4}} | collective-permute-start | bytes 25165832 | tf_op jit(solution)/shard_map/while/body/eval_jaxpr/ppermute | solution.py:104
  1202.4 121.9 %collective-permute-start = (bf16[2,16,256,4,128]{4,2,3,1,0:T(8,128)(2,1)}, bf16[2,16,256,4,128]{4,2,3,1,0:T(8,128)(2,1)}, u32[]{:S(2)}, u32[]{:S(2)}) collective-permute-start(bf16[2,16,256,4,128]{4,2,3,1,0:T(8,128)(2,1)} %get-tuple-element.529), channel_id=1, source_target_pairs={{0,1},{1,2},{2,3},{3,0},{4,5},{5,6},{6,7},{7,4}} | collective-permute-start | bytes 25165832 | tf_op jit(solution)/shard_map/while/body/eval_jaxpr/ppermute | solution.py:104
  1403.8 121.9 %collective-permute-start = (bf16[2,16,256,4,128]{4,2,3,1,0:T(8,128)(2,1)}, bf16[2,16,256,4,128]{4,2,3,1,0:T(8,128)(2,1)}, u32[]{:S(2)}, u32[]{:S(2)}) collective-permute-start(bf16[2,16,256,4,128]{4,2,3,1,0:T(8,128)(2,1)} %get-tuple-element.529), channel_id=1, source_target_pairs={{0,1},{1,2},{2,3},{3,0},{4,5},{5,6},{6,7},{7,4}} | collective-permute-start | bytes 25165832 | tf_op jit(solution)/shard_map/while/body/eval_jaxpr/ppermute | solution.py:104
Sparse Core Ops, SparseCore 0:
  8.9 484.1 all-gather.1
  1744.9 934.9 reduce-scatter.1
where the time goes:
time: 2730 us; the launch traced here: 2710 us
  waiting for transfers between devices  1710 us (63%)
  matrix products  539 us (20%)
  other arithmetic  221 us (8%)
  local copies, waits for them, and re-layouts  194 us (7%)
  starting transfers between devices  32.3 us (1%)
    reduce_scatter x1, waiting for transfers between devices, local_fn(): y_rows = lax.psum_scatter(partial_y, 'tp', scatter_dimension=1, tiled=True)  935 us
    all_gather x1, waiting for transfers between devices, local_fn(): x_pair = lax.all_gather(x_rows, 'tp', axis=1, tiled=True)  469 us
    ppermute x3, waiting for transfers between devices, kv_step(): kv_blk = lax.ppermute(kv_blk, 'cp', send_pairs)  304 us
    dot_general x1, matrix products, project_heads(): jnp.dot(x_rows, w_query, preferred_element_type=jnp.float32)  122 us
    dot_general x1, matrix products, project_out(): jnp.einsum('bhgqd,hgde->bqe', attn_out, w_out_heads, preferred_element_ty...  118 us
    dot_general x5, matrix products, block_scores(): jnp.einsum('bqhgd,bkhd->bhgqk', q_blk, k_blk, preferred_element_type=jnp....  106 us
    dot_general x3, matrix products, absorb(): jnp.einsum('bhgqk,bkhd->bhgqd', exp_scores.astype(jnp.bfloat16), v_blk, p...  92.5 us
    unnamed x18, local copies, waits for them, and re-layouts  56.8 us
  transfers between devices with their start and end apart: 5, of which 5 were waited for; matrix products, arithmetic and copies ran while one was open for 0% of the time, Pallas kernels for 0%

commit v1 on v0

v1 whole, which is shorter than its diff:
```python
import functools
import math
import jax
import jax.numpy as jnp
from jax import lax
from jax.experimental import pallas as pl
from jax.experimental.pallas import tpu as pltpu
from jax.sharding import PartitionSpec as P

HEAD_DIM = 128
ROPE_BASE = 500000
AXES = ('tp', 'cp')


def rope_tables(pos_vals):
    inv_freq = jnp.asarray([ROPE_BASE ** (-2.0 * freq_idx / HEAD_DIM) for freq_idx in range(HEAD_DIM // 2)], dtype=jnp.float32)
    angles = pos_vals.astype(jnp.float32)[..., None] * inv_freq
    cos_t, sin_t = jnp.cos(angles), jnp.sin(angles)
    return jnp.concatenate([cos_t, cos_t], axis=-1), jnp.concatenate([-sin_t, sin_t], axis=-1)


def rotate(head_vals, cos_t, sin_t):
    wide = head_vals.astype(jnp.float32)
    return (wide * cos_t + pltpu.roll(wide, HEAD_DIM // 2, 1) * sin_t).astype(jnp.bfloat16)


def rope_own_body(k_ref, v_ref, cos_ref, sin_ref, kv_ref):
    width = k_ref.shape[1]
    for col in range(0, width, HEAD_DIM):
        kv_ref[:, col:col + HEAD_DIM] = rotate(k_ref[:, col:col + HEAD_DIM], cos_ref[...], sin_ref[...])
    kv_ref[:, width:] = v_ref[...]


def rope_other_body(core_ref, near_ref, far_ref, cos_ref, sin_ref, kv_ref):
    width = near_ref.shape[1]
    half = width // 2
    for src_ref, slot in ((near_ref, core_ref[0]), (far_ref, 1 - core_ref[0])):
        for col in range(0, half, HEAD_DIM):
            at = pl.multiple_of(slot * half + col, HEAD_DIM)
            kv_ref[:, pl.ds(at, HEAD_DIM)] = rotate(src_ref[:, col:col + HEAD_DIM], cos_ref[...], sin_ref[...])
        at = pl.multiple_of(width + slot * half, HEAD_DIM)
        kv_ref[:, pl.ds(at, half)] = src_ref[:, half:]


def rope_own(k_proj, v_proj, cos_t, sin_t, block):
    rows, width = k_proj.shape
    spec = lambda cols: pl.BlockSpec((block, cols), lambda i: (i, 0))
    return pl.pallas_call(
        rope_own_body, grid=(rows // block,),
        in_specs=[spec(width), spec(width), spec(HEAD_DIM), spec(HEAD_DIM)], out_specs=spec(2 * width),
        out_shape=jax.ShapeDtypeStruct((rows, 2 * width), jnp.bfloat16),
        cost_estimate=pl.CostEstimate(flops=rows * width * 40, bytes_accessed=rows * width * 10, transcendentals=0),
        name='rope_own')(k_proj, v_proj, cos_t, sin_t)


def rope_other(core, near, far, cos_t, sin_t, block):
    rows, width = near.shape
    spec = lambda cols: pl.BlockSpec((block, cols), lambda i, *_: (i, 0))
    return pl.pallas_call(
        rope_other_body,
        grid_spec=pltpu.PrefetchScalarGridSpec(
            num_scalar_prefetch=1, grid=(rows // block,),
            in_specs=[spec(width), spec(width), spec(HEAD_DIM), spec(HEAD_DIM)], out_specs=spec(2 * width)),
        out_shape=jax.ShapeDtypeStruct((rows, 2 * width), jnp.bfloat16),
        cost_estimate=pl.CostEstimate(flops=rows * width * 40, bytes_accessed=rows * width * 10, transcendentals=0),
        name='rope_other')(core, near, far, cos_t, sin_t)


def attend_body(n_q, groups_each, q_per_kv, n_kv, flag_ref, *refs):
    q_refs = refs[:n_q]
    cos_ref, sin_ref = refs[n_q:n_q + 2]
    slots = refs[n_q + 2:n_q + 10]
    out_ref = refs[n_q + 10]
    s_refs = refs[n_q + 11:n_q + 13]
    p_refs = refs[n_q + 13:n_q + 15]
    block = cos_ref.shape[0]
    scale = 1.0 / math.sqrt(HEAD_DIM)
    kv_cols = n_kv * HEAD_DIM

    def run(use):
        keys = len(use) * block
        work = [(q_ref, idx) for q_ref in q_refs for idx in range(groups_each)]
        off = jnp.float32(-jnp.inf)
        bias_b = jnp.where(flag_ref[1] == 1, jnp.float32(0), off)
        bias_cd = jnp.where(flag_ref[2] == 1, jnp.float32(0), off)
        row_id = lax.broadcasted_iota(jnp.int32, (block, block), 0)
        col_id = lax.broadcasted_iota(jnp.int32, (block, block), 1)
        seen = col_id <= row_id

        def score(step):
            q_ref, idx = work[step]
            base = idx * q_per_kv * HEAD_DIM
            heads = [rotate(q_ref[:, base + h * HEAD_DIM:base + (h + 1) * HEAD_DIM], cos_ref[...], sin_ref[...]) for h in range(q_per_kv)]
            q_all = jnp.concatenate(heads, axis=0)
            at = pl.multiple_of(flag_ref[3 + step] * HEAD_DIM, HEAD_DIM)
            k_all = jnp.concatenate([slots[u][:, pl.ds(at, HEAD_DIM)] for u in use], axis=0)
            s_refs[step % 2][:, :keys] = lax.dot_general(q_all, k_all, (((1,), (1,)), ((), ())), preferred_element_type=jnp.float32)

        def soft(step):
            s_ref, p_ref = s_refs[step % 2], p_refs[step % 2]
            sums = []
            for h in range(q_per_kv):
                rows = slice(h * block, (h + 1) * block)
                tiles = []
                for n, u in enumerate(use):
                    tile = s_ref[rows, n * block:(n + 1) * block]
                    if u == 0:
                        tile = jnp.where(seen, tile, off)
                    elif u == 1:
                        tile = tile + bias_b
                    elif u in (2, 3):
                        tile = tile + bias_cd
                    tiles.append(tile)
                top = functools.reduce(jnp.maximum, tiles).max(axis=1, keepdims=True)
                total = None
                for n, tile in enumerate(tiles):
                    e = jnp.exp((tile - top) * scale)
                    total = e if total is None else total + e
                    p_ref[rows, n * block:(n + 1) * block] = e.astype(jnp.bfloat16)
                sums.append(total.sum(axis=1, keepdims=True))
            return sums

        def finish(step, sums):
            p_ref = p_refs[step % 2]
            at = pl.multiple_of(kv_cols + flag_ref[3 + step] * HEAD_DIM, HEAD_DIM)
            v_all = jnp.concatenate([slots[u][:, pl.ds(at, HEAD_DIM)] for u in use], axis=0)
            o_all = jnp.dot(p_ref[:, :keys], v_all, preferred_element_type=jnp.float32)
            for h in range(q_per_kv):
                col = (step * q_per_kv + h) * HEAD_DIM
                out_ref[:, col:col + HEAD_DIM] = (o_all[h * block:(h + 1) * block] / sums[h]).astype(jnp.bfloat16)

        score(0)
        for step in range(len(work)):
            if step + 1 < len(work):
                score(step + 1)
            sums = soft(step)
            finish(step, sums)

    @pl.when(flag_ref[0] == 1)
    def _():
        run((0, 1, 2, 3, 4, 5, 6, 7))

    @pl.when(flag_ref[0] == 0)
    def _():
        run((0, 1, 2, 3))


def attend(flags, q_list, cos_t, sin_t, slots, block, q_per_kv):
    rows = cos_t.shape[0]
    n_q = len(q_list)
    width = q_list[0].shape[1]
    groups_each = width // (q_per_kv * HEAD_DIM)
    n_kv = slots[0].shape[1] // (2 * HEAD_DIM)
    kv_width = slots[0].shape[1]
    here = lambda cols: pl.BlockSpec((block, cols), lambda i, f: (i, 0))
    gated = lambda idx: pl.BlockSpec((block, kv_width), lambda i, f: (i * f[idx], 0))
    slot_specs = [here(kv_width), gated(1), gated(2), gated(2), gated(0), gated(0), gated(0), gated(0)]
    stack = q_per_kv * block
    flops = 4 * rows * width * n_q * 8 * block
    return pl.pallas_call(
        functools.partial(attend_body, n_q, groups_each, q_per_kv, n_kv),
        grid_spec=pltpu.PrefetchScalarGridSpec(
            num_scalar_prefetch=1, grid=(rows // block,),
            in_specs=[here(width)] * n_q + [here(HEAD_DIM), here(HEAD_DIM)] + slot_specs,
            out_specs=here(width * n_q),
            scratch_shapes=[pltpu.VMEM((stack, 8 * block), jnp.float32)] * 2 + [pltpu.VMEM((stack, 8 * block), jnp.bfloat16)] * 2),
        out_shape=jax.ShapeDtypeStruct((rows, width * n_q), jnp.bfloat16),
        compiler_params=pltpu.CompilerParams(vmem_limit_bytes=56 * 1024 * 1024),
        cost_estimate=pl.CostEstimate(flops=flops * 2, bytes_accessed=rows * (width * n_q * 4 + 8 * kv_width * 2), transcendentals=rows * width * n_q * 8))(flags, *q_list, cos_t, sin_t, *slots)


def gather_dot_body(n_w, has_x, o_ref, *refs):
    w_refs = refs[:n_w]
    acc_ref = refs[n_w]
    out_ref = refs[-1]
    depth = w_refs[0].shape[0]
    rows = o_ref.shape[0]
    step = min(512, rows)
    for top in range(0, rows, step):
        part = slice(top, top + step)
        total = acc_ref[part, :]
        for j in range(n_w):
            total = total + jnp.dot(o_ref[part, j * depth:(j + 1) * depth], w_refs[j][...], preferred_element_type=jnp.float32)
        if has_x:
            total = refs[n_w + 1][part, :].astype(jnp.float32) + total
        out_ref[part, :] = total.astype(out_ref.dtype)


def gather_dot(o_vals, w_list, acc, x_rows):
    rows, depth_all = o_vals.shape
    depth, cols = w_list[0].shape
    tile = 512
    tall = pl.BlockSpec((rows, tile), lambda i: (0, i))
    args = [o_vals, *w_list, acc] + ([x_rows] if x_rows is not None else [])
    specs = [pl.BlockSpec((rows, depth_all), lambda i: (0, 0))] + [pl.BlockSpec((depth, tile), lambda i: (0, i))] * len(w_list) + [tall] * (len(args) - 1 - len(w_list))
    return pl.pallas_call(
        functools.partial(gather_dot_body, len(w_list), x_rows is not None),
        grid=(cols // tile,), in_specs=specs, out_specs=tall,
        out_shape=jax.ShapeDtypeStruct((rows, cols), jnp.float32 if x_rows is None else jnp.bfloat16),
        compiler_params=pltpu.CompilerParams(vmem_limit_bytes=58 * 1024 * 1024),
        cost_estimate=pl.CostEstimate(flops=2 * rows * depth_all * cols, bytes_accessed=rows * cols * 8, transcendentals=0))(*args)


def solution(mesh):
    cp_size = mesh.shape['cp']
    row_spec = P('data', ('cp', 'tp'))
    flat = lambda c, t: t * cp_size + c
    swap_y = [(flat(c, t), flat(c, 1 - t)) for c in range(cp_size) for t in range(2)]
    swap_x = [(flat(c, t), flat(c ^ 2, t)) for c in range(cp_size) for t in range(2)]
    swap_d = [(flat(c, t), flat(c ^ 1, t)) for c in range(cp_size) for t in range(2)]
    own_d = [(flat(0, 0), flat(1, 0)), (flat(2, 0), flat(3, 0)), (flat(1, 1), flat(0, 1)), (flat(3, 1), flat(2, 1))]
    own_x = [(flat(0, 0), flat(2, 0)), (flat(1, 0), flat(3, 0)), (flat(2, 1), flat(0, 1)), (flat(3, 1), flat(1, 1))]
    own_xd = [(flat(2, 0), flat(3, 0)), (flat(3, 0), flat(2, 0)), (flat(0, 1), flat(1, 1)), (flat(1, 1), flat(0, 1))]
    up_y = [(flat(c, 0), flat(c, 1)) for c in range(cp_size)]
    up_x = [(flat(c, 1), flat(c ^ 2, 1)) for c in range(cp_size)]
    up_d = [(flat(c, 1), flat(c ^ 1, 1)) for c in range(cp_size)]

    def move(vals, pairs):
        return lax.ppermute(vals, AXES, pairs)

    def after(vals, *others):
        return lax.optimization_barrier((vals, *others))[0]

    def block_fn(x_rows, pos_rows, w_query, w_key, w_value, w_out):
        batch, block, dim = x_rows.shape
        rows = batch * block
        kv_local = w_key.shape[1] // HEAD_DIM
        q_per_kv = w_query.shape[1] // w_key.shape[1]
        group = q_per_kv * HEAD_DIM
        c_idx, t_idx = lax.axis_index('cp'), lax.axis_index('tp')
        core = c_idx % 2
        x2 = x_rows.reshape(rows, dim)
        cos_t, sin_t = (tab.reshape(rows, HEAD_DIM) for tab in rope_tables(pos_rows))

        def project(weights):
            return jnp.dot(x2, weights, preferred_element_type=jnp.float32).astype(jnp.bfloat16)

        half = w_key.shape[1] // 2
        kv_send = jnp.concatenate([lax.dynamic_slice_in_dim(w_key, core * half, half, 1),
                                   lax.dynamic_slice_in_dim(w_value, core * half, half, 1)], axis=1)
        kv_near = move(kv_send, swap_y)

        kv_own = rope_own(project(w_key), project(w_value), cos_t, sin_t, block)
        q_own = project(w_query)
        kv_near = after(kv_near, q_own)
        kv_far = move(kv_near, swap_d)
        kv_oth = rope_other(core.reshape(1).astype(jnp.int32), project(kv_near), project(kv_far), cos_t, sin_t, block)

        c_own = move(kv_own, own_x)
        b_own = move(kv_own, own_d)
        d_own = move(c_own, own_xd)
        e_oth = move(kv_own, up_y)
        c_oth = move(kv_oth, own_x)
        b_oth = move(kv_oth, own_d)
        d_oth = move(c_oth, own_xd)
        e_own = move(kv_oth, up_y)
        f_oth = move(e_oth, up_d)
        g_oth = move(e_oth, up_x)
        h_oth = move(g_oth, up_d)
        f_own = move(e_own, up_d)
        g_own = move(e_own, up_x)
        h_own = move(g_own, up_d)
        slots_own = (kv_own, b_own, c_own, d_own, e_own, f_own, g_own, h_own)
        slots_oth = (kv_oth, b_oth, c_oth, d_oth, e_oth, f_oth, g_oth, h_oth)

        wq_send = lax.dynamic_slice_in_dim(w_query, c_idx * group, group, 1)
        wq0 = move(wq_send, swap_y)
        wq2 = move(wq0, swap_d)
        wq1 = move(wq0, swap_x)
        wq3 = move(wq1, swap_d)
        wo_send = lax.dynamic_slice_in_dim(w_out, c_idx * group, group, 0)
        wo0 = move(wo_send, swap_y)
        wo2 = move(wo0, swap_d)
        wo1 = move(wo0, swap_x)
        wo3 = move(wo1, swap_d)

        use_b = jnp.where(t_idx == 0, core, 1 - core)
        use_cd = jnp.where(t_idx == 0, c_idx // 2, 1 - c_idx // 2)
        head_flags = [t_idx, use_b, use_cd]
        flags = lambda *groups: jnp.stack([jnp.asarray(f, jnp.int32) for f in head_flags + list(groups)])

        o_own = attend(flags(*range(kv_local)), [q_own], cos_t, sin_t, slots_own, block, q_per_kv)
        acc = jnp.dot(o_own, w_out, preferred_element_type=jnp.float32)
        wq0, wq2, acc = lax.optimization_barrier((wq0, wq2, acc))
        o_near = attend(flags(c_idx, c_idx ^ 1), [project(wq0), project(wq2)], cos_t, sin_t, slots_oth, block, q_per_kv)
        acc = gather_dot(o_near, [wo0, wo2], acc, None)
        wq1, wq3, acc = lax.optimization_barrier((wq1, wq3, acc))
        q_far = [project(wq1), project(wq3)]
        o_far = attend(flags(c_idx ^ 2, c_idx ^ 3), q_far, cos_t, sin_t, slots_oth, block, q_per_kv)
        y_rows = gather_dot(o_far, [wo1, wo3], acc, x2)
        return y_rows.reshape(x_rows.shape)

    return jax.shard_map(block_fn, mesh=mesh,
                         in_specs=(row_spec, row_spec, P(None, 'tp'), P(None, 'tp'), P(None, 'tp'), P('tp', None)),
                         out_specs=row_spec, check_vma=False)
```

time: 2730 us -> 1420 us (0.52)
  the two profiles are of different devices: /device:TPU:0 before, /device:TPU:5 now
where the time goes in v1:
time: 1420 us; the launch traced here: 1410 us
  waiting for transfers between devices  763 us (54%)
  Pallas kernels  288 us (20%)
  matrix products  287 us (20%)
  starting transfers between devices  48.2 us (3%)
  local copies, waits for them, and re-layouts  14.9 us (1%)
    ppermute x24, waiting for transfers between devices, move(): return lax.ppermute(vals, AXES, pairs)  763 us
    dot_general x9, matrix products, project(): jnp.dot(x2, weights, preferred_element_type=jnp.float32)  222 us
    pallas_call x3, Pallas kernels, attend(): pl.pallas_call(functools.partial(attend_body, n_q, groups_each, q_per_kv,...  179 us
    pallas_call x2, Pallas kernels, gather_dot(): pl.pallas_call(functools.partial(gather_dot_body, len(w_list), x_rows is...  87.5 us
    dot_general x1, matrix products, block_fn(): acc = jnp.dot(o_own, w_out, preferred_element_type=jnp.float32)  64.8 us
    ppermute x24, starting transfers between devices, move(): return lax.ppermute(vals, AXES, pairs)  48.2 us
  transfers between devices with their start and end apart: 24, of which 6 were waited for; matrix products, arithmetic and copies ran while one was open for 21% of the time, Pallas kernels for 17%

profile of v1, /device:TPU:5, one launch (start us, length us, event | category | flops | bytes accessed | tf_op | source)
XLA Modules:
  0.0 1410.1 jit_solution(1810372477343672665)
XLA Ops:
  7.3 16.1 %convolution_convert_fusion.7.v_ref = bf16[2048,512]{1,0:T(8,128)(2,1)} fusion(bf16[2048,5120]{1,0:T(8,128)(2,1)} %bitcast.44, bf16[5120,512]{1,0:T(8,128)(2,1)S(1)} %bitcast.55), kind=kOutput, calls=%fused_computation.8 | convolution fusion | flops 10738466816 | bytes 28311552 | tf_op jit(solution)/shard_map/dot_general | solution.py:236
  23.4 3.7 fusion.6
  29.1 64.0 %convolution_convert_fusion.refs_0_ = bf16[2048,2560]{1,0:T(8,128)(2,1)} fusion(bf16[2048,5120]{1,0:T(8,128)(2,1)} %bitcast.45, bf16[5120,2560]{1,0:T(8,128)(2,1)} %param.9), kind=kOutput, calls=%fused_computation | convolution fusion | flops 53692334080 | bytes 57671680 | tf_op jit(solution)/shard_map/dot_general | solution.py:236
  93.1 27.1 %collective-permute-done.7 = bf16[5120,512]{1,0:T(8,128)(2,1)} collective-permute-done((bf16[5120,512]{1,0:T(8,128)(2,1)}, bf16[5120,512]{1,0:T(8,128)(2,1)}, u32[]{:S(2)}, u32[]{:S(2)}) %collective-permute-start.7) | collective-permute-done | bytes 5242912 | tf_op jit(solution)/shard_map/ppermute | solution.py:219
  121.8 17.6 %convolution_convert_fusion.8.k_ref = bf16[2048,512]{1,0:T(8,128)(2,1)} fusion(bf16[2048,5120]{1,0:T(8,128)(2,1)} %bitcast.46, bf16[5120,512]{1,0:T(8,128)(2,1)} %param.10), kind=kOutput, calls=%fused_computation.9 | convolution fusion | flops 10738466816 | bytes 28311552 | tf_op jit(solution)/shard_map/dot_general | solution.py:236
  139.3 11.1 rope_own.1.refs_3_
  151.8 17.8 %fusion.4.near_ref = bf16[2048,512]{1,0:T(8,128)(2,1)} fusion(bf16[2048,5120]{1,0:T(8,128)(2,1)} %bitcast.47, bf16[5120,512]{1,0:T(8,128)(2,1)} %collective-permute-done.7), kind=kOutput, calls=%fused_computation.14 | convolution fusion | flops 10738466816 | bytes 28311552 | tf_op jit(solution)/shard_map/dot_general | solution.py:236
  169.5 17.6 %fusion.5.far_ref = bf16[2048,512]{1,0:T(8,128)(2,1)} fusion(bf16[2048,5120]{1,0:T(8,128)(2,1)} %bitcast.48, bf16[5120,512]{1,0:T(8,128)(2,1)} %collective-permute-done.8), kind=kOutput, calls=%fused_computation.15 | convolution fusion | flops 10738466816 | bytes 28311552 | tf_op jit(solution)/shard_map/dot_general | solution.py:236
  187.1 11.2 rope_other.1.refs_4_
  199.5 3.5 constant_dynamic-slice_fusion.3
  203.0 6.0 collective-permute-start
  215.2 29.5 %collective-permute-done.5.refs_5_ = bf16[2048,1024]{1,0:T(8,128)(2,1)} collective-permute-done((bf16[2048,1024]{1,0:T(8,128)(2,1)}, bf16[2048,1024]{1,0:T(8,128)(2,1)}, u32[]{:S(2)}, u32[]{:S(2)}) %collective-permute-start.5) | collective-permute-done | bytes 4194336 | tf_op jit(solution)/shard_map/ppermute | solution.py:219
  246.1 48.5 %collective-permute-done.9.refs_7_ = bf16[2048,1024]{1,0:T(8,128)(2,1)} collective-permute-done((bf16[2048,1024]{1,0:T(8,128)(2,1)}, bf16[2048,1024]{1,0:T(8,128)(2,1)}, u32[]{:S(2)}, u32[]{:S(2)}) %collective-permute-start.9) | collective-permute-done | bytes 4194336 | tf_op jit(solution)/shard_map/ppermute | solution.py:219
  294.6 3.6 collective-permute-start.11
  298.2 4.1 collective-permute-start.6
  302.3 363.0 %collective-permute-done.16.refs_8_ = bf16[2048,1024]{1,0:T(8,128)(2,1)} collective-permute-done((bf16[2048,1024]{1,0:T(8,128)(2,1)S(1)}, bf16[2048,1024]{1,0:T(8,128)(2,1)}, u32[]{:S(2)}, u32[]{:S(2)}) %collective-permute-start.16) | collective-permute-done | bytes 4194336 | tf_op jit(solution)/shard_map/ppermute | solution.py:219
  665.3 3.6 collective-permute-start.18
  669.0 3.3 collective-permute-start.10
  679.0 80.1 %collective-permute-done.18.refs_10_ = bf16[2048,1024]{1,0:T(8,128)(2,1)} collective-permute-done((bf16[2048,1024]{1,0:T(8,128)(2,1)}, bf16[2048,1024]{1,0:T(8,128)(2,1)}, u32[]{:S(2)}, u32[]{:S(2)}) %collective-permute-start.18) | collective-permute-done | bytes 4194336 | tf_op jit(solution)/shard_map/ppermute | solution.py:219
  760.6 4.2 collective-permute-start.19
  764.8 82.8 %shard_map.73 = bf16[2048,2560]{1,0:T(8,128)(2,1)} custom-call(s32[7]{0:T(128)} %stack.45.flag_ref, bf16[2048,2560]{1,0:T(8,128)(2,1)} %convolution_convert_fusion.refs_0_, f32[2048,128]{1,0:T(8,128)} %get-tuple-element.22.cos_ref.refs_1_.refs_2_, f32[2048,128]{1,0:T(8,128)} %get-tuple-element.23.sin_ref.refs_2_.refs_3_, ...), custom_call_target="tpu_custom_call" | custom-call | flops 42949672960 | bytes 54525952 | tf_op jit(solution)/shard_map/pallas_call | solution.py:160
  848.8 64.8 %fusion.7.refs_2_ = f32[2048,5120]{1,0:T(8,128)} fusion(bf16[2048,2560]{1,0:T(8,128)(2,1)} %shard_map.73, bf16[2560,5120]{1,0:T(8,128)(2,1)} %param.12), kind=kOutput, calls=%fused_computation.26 | convolution fusion | flops 53687091200 | bytes 78643200 | tf_op jit(solution)/shard_map/dot_general | solution.py:283
  916.3 214.3 %collective-permute-done.14.refs_6_ = bf16[2048,1024]{1,0:T(8,128)(2,1)S(1)} collective-permute-done((bf16[2048,1024]{1,0:T(8,128)(2,1)S(1)}, bf16[2048,1024]{1,0:T(8,128)(2,1)S(1)}, u32[]{:S(2)}, u32[]{:S(2)}) %collective-permute-start.14) | collective-permute-done | bytes 4194336 | tf_op jit(solution)/shard_map/ppermute | solution.py:219
  1130.6 4.5 collective-permute-start.15
  1135.1 22.4 %fusion.refs_0_ = bf16[2048,640]{1,0:T(8,128)(2,1)} fusion(bf16[2048,5120]{1,0:T(8,128)(2,1)} %bitcast.49, bf16[5120,640]{1,0:T(8,128)(2,1)} %collective-permute-done), kind=kOutput, calls=%fused_computation.10 | convolution fusion | flops 13423083520 | bytes 30146560 | tf_op jit(solution)/shard_map/dot_general | solution.py:236
  1157.5 22.2 %fusion.1.refs_1_ = bf16[2048,640]{1,0:T(8,128)(2,1)} fusion(bf16[2048,5120]{1,0:T(8,128)(2,1)} %bitcast.50, bf16[5120,640]{1,0:T(8,128)(2,1)} %collective-permute-done.3), kind=kOutput, calls=%fused_computation.11 | convolution fusion | flops 13423083520 | bytes 30146560 | tf_op jit(solution)/shard_map/dot_general | solution.py:236
  1182.2 47.8 %shard_map.74.o_ref = bf16[2048,1280]{1,0:T(8,128)(2,1)} custom-call(s32[5]{0:T(128)} %stack.44.flag_ref, bf16[2048,640]{1,0:T(8,128)(2,1)} %fusion.refs_0_, bf16[2048,640]{1,0:T(8,128)(2,1)} %fusion.1.refs_1_, f32[2048,128]{1,0:T(8,128)} %get-tuple-element.22.cos_ref.refs_1_.refs_2_, f32[2048,128]{1,0:T(8,128)} %get-tuple-element.23.sin_ref.refs_2_.refs_3_, ...), custom_call_target="tpu_custom_call" | custom-call | flops 21474836480 | bytes 44040192 | tf_op jit(solution)/shard_map/pallas_call | solution.py:160
  1229.9 44.2 %shard_map.75.refs_2_ = f32[2048,5120]{1,0:T(8,128)} custom-call(bf16[2048,1280]{1,0:T(8,128)(2,1)} %shard_map.74.o_ref, bf16[640,5120]{1,0:T(8,128)(2,1)} %collective-permute-done.20.refs_0_, bf16[640,5120]{1,0:T(8,128)(2,1)} %collective-permute-done.21.refs_1_, f32[2048,5120]{1,0:T(8,128)} %fusion.7.refs_2_), custom_call_target="tpu_custom_call" | custom-call | flops 26843545600 | bytes 83886080 | tf_op jit(solution)/shard_map/pallas_call | solution.py:196
  1274.1 22.2 %fusion.2.refs_0_ = bf16[2048,640]{1,0:T(8,128)(2,1)} fusion(bf16[2048,5120]{1,0:T(8,128)(2,1)} %bitcast.51, bf16[5120,640]{1,0:T(8,128)(2,1)} %collective-permute-done.1), kind=kOutput, calls=%fused_computation.12 | convolution fusion | flops 13423083520 | bytes 30146560 | tf_op jit(solution)/shard_map/dot_general | solution.py:236
  1296.3 22.2 %fusion.3.refs_1_ = bf16[2048,640]{1,0:T(8,128)(2,1)} fusion(bf16[2048,5120]{1,0:T(8,128)(2,1)} %bitcast.52, bf16[5120,640]{1,0:T(8,128)(2,1)} %collective-permute-done.2), kind=kOutput, calls=%fused_computation.13 | convolution fusion | flops 13423083520 | bytes 30146560 | tf_op jit(solution)/shard_map/dot_general | solution.py:236
  1318.5 48.1 %shard_map.76.o_ref = bf16[2048,1280]{1,0:T(8,128)(2,1)} custom-call(s32[5]{0:T(128)} %stack.41.flag_ref, bf16[2048,640]{1,0:T(8,128)(2,1)} %fusion.2.refs_0_, bf16[2048,640]{1,0:T(8,128)(2,1)} %fusion.3.refs_1_, f32[2048,128]{1,0:T(8,128)} %get-tuple-element.22.cos_ref.refs_1_.refs_2_, f32[2048,128]{1,0:T(8,128)} %get-tuple-element.23.sin_ref.refs_2_.refs_3_, ...), custom_call_target="tpu_custom_call" | custom-call | flops 21474836480 | bytes 44040192 | tf_op jit(solution)/shard_map/pallas_call | solution.py:160
  1366.5 43.3 %shard_map.77 = bf16[2048,5120]{1,0:T(8,128)(2,1)} custom-call(bf16[2048,1280]{1,0:T(8,128)(2,1)} %shard_map.76.o_ref, bf16[640,5120]{1,0:T(8,128)(2,1)} %collective-permute-done.22.refs_0_, bf16[640,5120]{1,0:T(8,128)(2,1)} %collective-permute-done.23.refs_1_, f32[2048,5120]{1,0:T(8,128)} %shard_map.75.refs_2_, bf16[2048,5120]{1,0:T(8,128)(2,1)} %bitcast.53), custom_call_target="tpu_custom_call" | custom-call | flops 26843545600 | bytes 83886080 | tf_op jit(solution)/shard_map/pallas_call | solution.py:196
  (62 shorter events, 35.3 us)
Async XLA Ops:
  2.9 3.1 copy-start.2
  2.9 4.1 slice-start
  2.9 4.4 slice-start.1
  6.0 114.2 %collective-permute-start.7 = (bf16[5120,512]{1,0:T(8,128)(2,1)}, bf16[5120,512]{1,0:T(8,128)(2,1)}, u32[]{:S(2)}, u32[]{:S(2)}) collective-permute-start(bf16[5120,512]{1,0:T(8,128)(2,1)} %pad_maximum_fusion), channel_id=1, source_target_pairs={{0,4},{4,0},{1,5},{5,1},{2,6},{6,2},{3,7},{7,3}} | collective-permute-start | bytes 15728648 | tf_op jit(solution)/shard_map/ppermute | solution.py:219
  7.3 16.1 %copy-start.3 = (f32[64]{0:T(128)S(1)}, f32[64]{0:T(128)}, u32[]{:S(2)}) copy-start(f32[64]{0:T(128)} %constant.57.clone) | copy-start | bytes 772
  120.2 49.3 %collective-permute-start.8 = (bf16[5120,512]{1,0:T(8,128)(2,1)}, bf16[5120,512]{1,0:T(8,128)(2,1)}, u32[]{:S(2)}, u32[]{:S(2)}) collective-permute-start(bf16[5120,512]{1,0:T(8,128)(2,1)} %collective-permute-done.7), channel_id=1, source_target_pairs={{0,1},{4,5},{1,0},{5,4},{2,3},{6,7},{3,2},{7,6}} | collective-permute-start | bytes 15728648 | tf_op jit(solution)/shard_map/ppermute | solution.py:219
  150.5 94.3 %collective-permute-start.5 = (bf16[2048,1024]{1,0:T(8,128)(2,1)}, bf16[2048,1024]{1,0:T(8,128)(2,1)}, u32[]{:S(2)}, u32[]{:S(2)}) collective-permute-start(bf16[2048,1024]{1,0:T(8,128)(2,1)} %rope_own.1.refs_3_), channel_id=1, source_target_pairs={{0,2},{1,3},{6,4},{7,5}} | collective-permute-start | bytes 12582920 | tf_op jit(solution)/shard_map/ppermute | solution.py:219
  198.3 96.3 %collective-permute-start.9 = (bf16[2048,1024]{1,0:T(8,128)(2,1)}, bf16[2048,1024]{1,0:T(8,128)(2,1)}, u32[]{:S(2)}, u32[]{:S(2)}) collective-permute-start(bf16[2048,1024]{1,0:T(8,128)(2,1)} %rope_other.1.refs_4_), channel_id=1, source_target_pairs={{0,4},{1,5},{2,6},{3,7}} | collective-permute-start | bytes 12582920 | tf_op jit(solution)/shard_map/ppermute | solution.py:219
  203.0 9.6 copy-start.1
  203.0 466.0 %collective-permute-start = (bf16[5120,640]{1,0:T(8,128)(2,1)S(1)}, bf16[5120,640]{1,0:T(8,128)(2,1)}, u32[]{:S(2)}, u32[]{:S(2)}) collective-permute-start(bf16[5120,640]{1,0:T(8,128)(2,1)S(1)} %constant_dynamic-slice_fusion.3), channel_id=1, source_target_pairs={{0,4},{4,0},{1,5},{5,1},{2,6},{6,2},{3,7},{7,3}} | collective-permute-start | bytes 19660808 | tf_op jit(solution)/shard_map/ppermute | solution.py:219
  212.4 461.9 %collective-permute-start.20 = (bf16[640,5120]{1,0:T(8,128)(2,1)S(1)}, bf16[640,5120]{1,0:T(8,128)(2,1)}, u32[]{:S(2)}, u32[]{:S(2)}) collective-permute-start(bf16[640,5120]{1,0:T(8,128)(2,1)S(1)} %constant_dynamic-slice_fusion), channel_id=1, source_target_pairs={{0,4},{4,0},{1,5},{5,1},{2,6},{6,2},{3,7},{7,3}} | collective-permute-start | bytes 19660808 | tf_op jit(solution)/shard_map/ppermute | solution.py:219
  212.6 85.6 %collective-permute-start.4 = (bf16[2048,1024]{1,0:T(8,128)(2,1)S(1)}, bf16[2048,1024]{1,0:T(8,128)(2,1)S(1)}, u32[]{:S(2)}, u32[]{:S(2)}) collective-permute-start(bf16[2048,1024]{1,0:T(8,128)(2,1)S(1)} %copy-done.1), channel_id=1, source_target_pairs={{0,1},{2,3},{5,4},{7,6}} | collective-permute-start | bytes 12582920 | tf_op jit(solution)/shard_map/ppermute | solution.py:219
  244.8 420.6 %collective-permute-start.16 = (bf16[2048,1024]{1,0:T(8,128)(2,1)S(1)}, bf16[2048,1024]{1,0:T(8,128)(2,1)}, u32[]{:S(2)}, u32[]{:S(2)}) collective-permute-start(bf16[2048,1024]{1,0:T(8,128)(2,1)S(1)} %copy-done.1), channel_id=1, source_target_pairs={{0,4},{1,5},{2,6},{3,7}} | collective-permute-start | bytes 12582920 | tf_op jit(solution)/shard_map/ppermute | solution.py:219
  294.6 377.8 %collective-permute-start.11 = (bf16[2048,1024]{1,0:T(8,128)(2,1)}, bf16[2048,1024]{1,0:T(8,128)(2,1)}, u32[]{:S(2)}, u32[]{:S(2)}) collective-permute-start(bf16[2048,1024]{1,0:T(8,128)(2,1)} %collective-permute-done.9.refs_7_), channel_id=1, source_target_pairs={{4,6},{5,7},{6,4},{7,5}} | collective-permute-start | bytes 12582920 | tf_op jit(solution)/shard_map/ppermute | solution.py:219
  298.2 376.1 %copy-start.4 = (bf16[2048,1024]{1,0:T(8,128)(2,1)}, bf16[2048,1024]{1,0:T(8,128)(2,1)S(1)}, u32[]{:S(2)}) copy-start(bf16[2048,1024]{1,0:T(8,128)(2,1)S(1)} %collective-permute-done.4.refs_4_) | copy-start | bytes 12582916
  298.2 378.5 %collective-permute-start.6 = (bf16[2048,1024]{1,0:T(8,128)(2,1)}, bf16[2048,1024]{1,0:T(8,128)(2,1)}, u32[]{:S(2)}, u32[]{:S(2)}) collective-permute-start(bf16[2048,1024]{1,0:T(8,128)(2,1)} %collective-permute-done.5.refs_5_), channel_id=1, source_target_pairs={{2,3},{3,2},{4,5},{5,4}} | collective-permute-start | bytes 12582920 | tf_op jit(solution)/shard_map/ppermute | solution.py:219
  665.3 93.7 %collective-permute-start.18 = (bf16[2048,1024]{1,0:T(8,128)(2,1)}, bf16[2048,1024]{1,0:T(8,128)(2,1)}, u32[]{:S(2)}, u32[]{:S(2)}) collective-permute-start(bf16[2048,1024]{1,0:T(8,128)(2,1)} %collective-permute-done.16.refs_8_), channel_id=1, source_target_pairs={{4,6},{5,7},{6,4},{7,5}} | collective-permute-start | bytes 12582920 | tf_op jit(solution)/shard_map/ppermute | solution.py:219
  669.0 91.3 %collective-permute-start.10 = (bf16[2048,1024]{1,0:T(8,128)(2,1)}, bf16[2048,1024]{1,0:T(8,128)(2,1)}, u32[]{:S(2)}, u32[]{:S(2)}) collective-permute-start(bf16[2048,1024]{1,0:T(8,128)(2,1)} %collective-permute-done.9.refs_7_), channel_id=1, source_target_pairs={{4,5},{5,4},{6,7},{7,6}} | collective-permute-start | bytes 12582920 | tf_op jit(solution)/shard_map/ppermute | solution.py:219
  672.4 88.2 %collective-permute-start.12 = (bf16[2048,1024]{1,0:T(8,128)(2,1)}, bf16[2048,1024]{1,0:T(8,128)(2,1)}, u32[]{:S(2)}, u32[]{:S(2)}) collective-permute-start(bf16[2048,1024]{1,0:T(8,128)(2,1)} %collective-permute-done.11.refs_9_), channel_id=1, source_target_pairs={{4,5},{5,4},{6,7},{7,6}} | collective-permute-start | bytes 12582920 | tf_op jit(solution)/shard_map/ppermute | solution.py:219
  674.3 173.2 %collective-permute-start.3 = (bf16[5120,640]{1,0:T(8,128)(2,1)}, bf16[5120,640]{1,0:T(8,128)(2,1)}, u32[]{:S(2)}, u32[]{:S(2)}) collective-permute-start(bf16[5120,640]{1,0:T(8,128)(2,1)} %collective-permute-done), channel_id=1, source_target_pairs={{0,1},{4,5},{1,0},{5,4},{2,3},{6,7},{3,2},{7,6}} | collective-permute-start | bytes 19660808 | tf_op jit(solution)/shard_map/ppermute | solution.py:219
  676.8 170.8 %copy-start = (bf16[2048,1024]{1,0:T(8,128)(2,1)S(1)}, bf16[2048,1024]{1,0:T(8,128)(2,1)}, u32[]{:S(2)}) copy-start(bf16[2048,1024]{1,0:T(8,128)(2,1)} %rope_other.1.refs_4_) | copy-start | bytes 12582916
  676.8 236.8 %collective-permute-start.17 = (bf16[2048,1024]{1,0:T(8,128)(2,1)}, bf16[2048,1024]{1,0:T(8,128)(2,1)}, u32[]{:S(2)}, u32[]{:S(2)}) collective-permute-start(bf16[2048,1024]{1,0:T(8,128)(2,1)} %collective-permute-done.16.refs_8_), channel_id=1, source_target_pairs={{4,5},{5,4},{6,7},{7,6}} | collective-permute-start | bytes 12582920 | tf_op jit(solution)/shard_map/ppermute | solution.py:219
  759.1 398.4 %collective-permute-start.1 = (bf16[5120,640]{1,0:T(8,128)(2,1)}, bf16[5120,640]{1,0:T(8,128)(2,1)}, u32[]{:S(2)}, u32[]{:S(2)}) collective-permute-start(bf16[5120,640]{1,0:T(8,128)(2,1)} %collective-permute-done), channel_id=1, source_target_pairs={{0,2},{4,6},{1,3},{5,7},{2,0},{6,4},{3,1},{7,5}} | collective-permute-start | bytes 19660808 | tf_op jit(solution)/shard_map/ppermute | solution.py:219
  760.3 419.4 %collective-permute-start.22 = (bf16[640,5120]{1,0:T(8,128)(2,1)}, bf16[640,5120]{1,0:T(8,128)(2,1)}, u32[]{:S(2)}, u32[]{:S(2)}) collective-permute-start(bf16[640,5120]{1,0:T(8,128)(2,1)} %collective-permute-done.20.refs_0_), channel_id=1, source_target_pairs={{0,2},{4,6},{1,3},{5,7},{2,0},{6,4},{3,1},{7,5}} | collective-permute-start | bytes 19660808 | tf_op jit(solution)/shard_map/ppermute | solution.py:219
  760.6 153.1 %collective-permute-start.19 = (bf16[2048,1024]{1,0:T(8,128)(2,1)}, bf16[2048,1024]{1,0:T(8,128)(2,1)}, u32[]{:S(2)}, u32[]{:S(2)}) collective-permute-start(bf16[2048,1024]{1,0:T(8,128)(2,1)} %collective-permute-done.18.refs_10_), channel_id=1, source_target_pairs={{4,5},{5,4},{6,7},{7,6}} | collective-permute-start | bytes 12582920 | tf_op jit(solution)/shard_map/ppermute | solution.py:219
  847.5 283.0 %collective-permute-start.14 = (bf16[2048,1024]{1,0:T(8,128)(2,1)S(1)}, bf16[2048,1024]{1,0:T(8,128)(2,1)S(1)}, u32[]{:S(2)}, u32[]{:S(2)}) collective-permute-start(bf16[2048,1024]{1,0:T(8,128)(2,1)S(1)} %copy-done), channel_id=1, source_target_pairs={{0,2},{1,3},{6,4},{7,5}} | collective-permute-start | bytes 12582920 | tf_op jit(solution)/shard_map/ppermute | solution.py:219
  913.6 316.3 %collective-permute-start.21 = (bf16[640,5120]{1,0:T(8,128)(2,1)}, bf16[640,5120]{1,0:T(8,128)(2,1)}, u32[]{:S(2)}, u32[]{:S(2)}) collective-permute-start(bf16[640,5120]{1,0:T(8,128)(2,1)} %collective-permute-done.20.refs_0_), channel_id=1, source_target_pairs={{0,1},{4,5},{1,0},{5,4},{2,3},{6,7},{3,2},{7,6}} | collective-permute-start | bytes 19660808 | tf_op jit(solution)/shard_map/ppermute | solution.py:219
  913.6 266.5 %collective-permute-start.13 = (bf16[2048,1024]{1,0:T(8,128)(2,1)S(1)}, bf16[2048,1024]{1,0:T(8,128)(2,1)S(1)}, u32[]{:S(2)}, u32[]{:S(2)}) collective-permute-start(bf16[2048,1024]{1,0:T(8,128)(2,1)S(1)} %copy-done), channel_id=1, source_target_pairs={{0,1},{2,3},{5,4},{7,6}} | collective-permute-start | bytes 12582920 | tf_op jit(solution)/shard_map/ppermute | solution.py:219
  1130.6 26.9 %copy-start.5 = (bf16[2048,1024]{1,0:T(8,128)(2,1)}, bf16[2048,1024]{1,0:T(8,128)(2,1)S(1)}, u32[]{:S(2)}) copy-start(bf16[2048,1024]{1,0:T(8,128)(2,1)S(1)} %collective-permute-done.14.refs_6_) | copy-start | bytes 12582916
  1130.6 51.6 %collective-permute-start.15 = (bf16[2048,1024]{1,0:T(8,128)(2,1)S(1)}, bf16[2048,1024]{1,0:T(8,128)(2,1)}, u32[]{:S(2)}, u32[]{:S(2)}) collective-permute-start(bf16[2048,1024]{1,0:T(8,128)(2,1)S(1)} %collective-permute-done.14.refs_6_), channel_id=1, source_target_pairs={{2,3},{3,2},{4,5},{5,4}} | collective-permute-start | bytes 12582920 | tf_op jit(solution)/shard_map/ppermute | solution.py:219
  1157.4 116.7 %collective-permute-start.2 = (bf16[5120,640]{1,0:T(8,128)(2,1)}, bf16[5120,640]{1,0:T(8,128)(2,1)}, u32[]{:S(2)}, u32[]{:S(2)}) collective-permute-start(bf16[5120,640]{1,0:T(8,128)(2,1)} %collective-permute-done.1), channel_id=1, source_target_pairs={{0,1},{4,5},{1,0},{5,4},{2,3},{6,7},{3,2},{7,6}} | collective-permute-start | bytes 19660808 | tf_op jit(solution)/shard_map/ppermute | solution.py:219
  1179.7 186.9 %collective-permute-start.23 = (bf16[640,5120]{1,0:T(8,128)(2,1)}, bf16[640,5120]{1,0:T(8,128)(2,1)}, u32[]{:S(2)}, u32[]{:S(2)}) collective-permute-start(bf16[640,5120]{1,0:T(8,128)(2,1)} %collective-permute-done.22.refs_0_), channel_id=1, source_target_pairs={{0,1},{4,5},{1,0},{5,4},{2,3},{6,7},{3,2},{7,6}} | collective-permute-start | bytes 19660808 | tf_op jit(solution)/shard_map/ppermute | solution.py:219
  (1 other events, 2.0 us)
